TPU v7x, 32 devices: a whole 2x2x4 slice. The times are simulated.
32 devices in a mesh: gx: 4 (over y, x), gy: 2 (over core), gz: 4 (over z).
Axes of the slice: x: 2, y: 2, z: 4, core: 2. Of those that a mesh axis runs over, the one named last changes fastest.
Arguments:
- measures: float32 [65536, 256], P(('gx', 'gy', 'gz')), may hold values from -6 to 6
- group_index: int32 [65536], P(('gx', 'gy', 'gz')), may hold values from 0 to 511, as said below
- distinct_keys: int32 [32, 512], P(('gx', 'gy', 'gz')), may hold values from 32 to 65567, as said below
- group_counts: int32 [32], P(('gx', 'gy', 'gz')), may hold values from 128 to 512, as said below
Outputs:
- group_sums: float32 [16384, 256], P(('gx', 'gy', 'gz'))
- group_rows: int32 [16384], P(('gx', 'gy', 'gz'))
- group_keys: int32 [16384], P(('gx', 'gy', 'gz'))
- group_total: int32 [], replicated
Inputs may be any that keep to these rules, and one draw needn't show every extreme that they name: `group_counts`: every device has between 128 and 512 groups, and some device has exactly 512. `group_index`: each row's index lies below its device's group count, and every group of a device has at least one row. `distinct_keys`: each device's keys rise strictly; all keys of device d equal d modulo 32, so no key lives on two devices; entries at and past the device's count are unused.
All inputs are finite; a program needn't handle non-finite values.
Results may differ from a plain program's by a relative error of at most 0.0003.
Values sent between devices are 32-bit elements; how exact they have to be, the bound alone decides.
A program may use at most 64 MiB of HBM per device.

v0:
```python
import jax
import jax.numpy as jnp
from jax import lax
from jax.sharding import PartitionSpec as P


def shards(measures, group_index, distinct_keys, group_counts):
    rows, width = measures.shape
    span = distinct_keys.shape[1]
    devices = lax.axis_size(("gx", "gy", "gz"))
    slots = span // devices
    plane = lax.axis_size("gx") * lax.axis_size("gy")
    line = lax.axis_size("gz")
    count = group_counts[0]
    myself = jnp.int32(0)
    sender_counts = lax.all_gather(group_counts, ("gx", "gy", "gz"), axis=0, tiled=True)
    sender_offsets = jnp.cumsum(sender_counts) - sender_counts
    myself = lax.axis_index(("gx", "gy", "gz"))
    offset = sender_offsets[myself]
    group_total = jnp.sum(sender_counts)
    block = min(1024, rows)
    labels = lax.broadcasted_iota(jnp.int32, (span, block), 0)

    def accumulate(step, carry):
        totals, tallies = carry
        start = step * block
        index = lax.dynamic_slice_in_dim(group_index, start, block)
        values = lax.dynamic_slice_in_dim(measures, start, block, 0)
        hits = index[None, :] == labels
        totals = totals + jnp.dot(
            hits.astype(jnp.float32),
            values,
            precision=lax.Precision.HIGHEST,
            preferred_element_type=jnp.float32,
        )
        tallies = tallies + jnp.sum(hits, axis=1, dtype=jnp.int32)
        return (totals, tallies)

    sums, tallies = lax.fori_loop(
        0,
        rows // block,
        accumulate,
        (jnp.zeros((span, width), jnp.float32), jnp.zeros((span,), jnp.int32)),
    )
    local = jnp.arange(span, dtype=jnp.int32)
    live = local < count
    keys = jnp.where(live, distinct_keys[0], -1)
    fields = jnp.stack([tallies.astype(jnp.float32), keys.astype(jnp.float32)], axis=1)
    extra = fields.shape[1]

    def arrange(array):
        shaped = array.reshape((slots, devices) + array.shape[1:])
        rolled = jnp.roll(shaped, offset, axis=1)
        return rolled.reshape((slots, plane, line) + array.shape[1:])

    outgoing = (arrange(sums), arrange(fields))
    arrived = (
        lax.all_to_all(
            lax.all_to_all(outgoing[0], "gz", split_axis=2, concat_axis=2, tiled=True),
            ("gx", "gy"),
            split_axis=1,
            concat_axis=1,
            tiled=True,
        ),
        lax.all_to_all(
            lax.all_to_all(outgoing[1], "gz", split_axis=2, concat_axis=2, tiled=True),
            ("gx", "gy"),
            split_axis=1,
            concat_axis=1,
            tiled=True,
        ),
    )
    got_sums, got_fields = arrived
    got_fields = got_fields.reshape(-1, extra)
    sender = jnp.arange(devices, dtype=jnp.int32).reshape(1, plane, line)
    start_of = sender_offsets.reshape(1, plane, line)
    count_of = sender_counts.reshape(1, plane, line)
    level = jnp.arange(slots, dtype=jnp.int32).reshape(slots, 1, 1)
    position = level * devices + (myself - start_of) % devices
    arrived_live = (position < count_of) & (sender >= 0)
    target = jnp.where(arrived_live, (start_of + position) // devices, span).reshape(-1)
    group_sums = (
        jnp.zeros((span, width), jnp.float32)
        .at[target]
        .set(got_sums.reshape(-1, width), mode="drop")
    )
    group_rows = (
        jnp.zeros((span,), jnp.int32)
        .at[target]
        .set(got_fields[:, 0].astype(jnp.int32), mode="drop")
    )
    group_keys = (
        jnp.full((span,), -1, jnp.int32)
        .at[target]
        .set(got_fields[:, 1].astype(jnp.int32), mode="drop")
    )
    return (group_sums, group_rows, group_keys, group_total)


def solution(mesh):
    return jax.shard_map(
        shards,
        mesh=mesh,
        in_specs=(
            P(("gx", "gy", "gz"), None),
            P(("gx", "gy", "gz")),
            P(("gx", "gy", "gz"), None),
            P(("gx", "gy", "gz")),
        ),
        out_specs=(P(("gx", "gy", "gz"), None), P(("gx", "gy", "gz")), P(("gx", "gy", "gz")), P()),
        check_vma=False,
    )
```

profile of v0, /device:TPU:0, one launch (start us, length us, event | category | flops | bytes accessed | tf_op | source)
XLA Modules:
  0.0 106.3 jit_solution(15189355763401430567)
XLA Ops:
  1.4 42.0 %all-reduce = s32[32]{0:T(128)S(1)} all-reduce(s32[32]{0:T(128)S(1)} %dynamic-update-slice), channel_id=1, replica_groups=mesh['gx'=4,'gy'=2,'gz'=4] {'gx','gy','gz'}, use_global_device_ids=true, to_apply=%add | all-reduce | flops 32 | bytes 256
  46.8 7.4 %while.16 = (s32[]{:T(128)}, f32[512,256]{1,0:T(8,128)S(1)}, s32[512]{0:T(512)S(1)}, s32[2048]{0:T(1024)}, f32[2048,256]{1,0:T(8,128)}, /*index=5*/s32[]{:T(128)}, s32[]{:T(128)}, s32[]{:T(128)}, s32[]{:T(128)}) while((s32[]{:T(128)}, f32[512,256]{1,0:T(8,128)S(1)}, s32[512]{0:T(512)S(1)}, s32[2048]{0:T(1024)}, ...), condition=%wide.region_3.4_spmd.clone, body=%wide.region_1.3_spmd.clone.sunk | while | flops 1612972544 | bytes 2121886 | solution.py:39
  46.9 0.7 dynamic_slice.55
  47.6 2.7 %fusion.24 = f32[512,256]{1,0:T(8,128)S(1)} fusion(f32[2048,256]{1,0:T(8,128)} %get-tuple-element.203, s32[]{:T(128)S(6)} %select_n.107, s32[1024]{0:T(1024)S(1)} %dynamic_slice.55, f32[512,256]{1,0:T(8,128)S(1)} %get-tuple-element.191, pred[]{:T(512)S(6)} %compare.20), kind=kOutput, calls=%fused_computation.8.clone.1 | convolution fusion | flops 1611399168 | bytes 2101253 | tf_op jit(solution)/shard_map/while/body/eval_jaxpr/dot_general | solution.py:30
  50.6 0.7 dynamic_slice.55
  51.2 2.7 %fusion.24 = f32[512,256]{1,0:T(8,128)S(1)} fusion(f32[2048,256]{1,0:T(8,128)} %get-tuple-element.203, s32[]{:T(128)S(6)} %select_n.107, s32[1024]{0:T(1024)S(1)} %dynamic_slice.55, f32[512,256]{1,0:T(8,128)S(1)} %get-tuple-element.191, pred[]{:T(512)S(6)} %compare.20), kind=kOutput, calls=%fused_computation.8.clone.1 | convolution fusion | flops 1611399168 | bytes 2101253 | tf_op jit(solution)/shard_map/while/body/eval_jaxpr/dot_general | solution.py:30
  54.8 0.7 reduce.5
  55.8 0.7 reshape.312
  56.5 3.6 %all-to-all-start.2 = ((f32[4,1,256]{2,1,0:T(1,128)}), f32[4,1,256]{2,1,0:T(1,128)S(1)}, u32[]{:S(2)}, u32[]{:S(2)}) async-start(f32[4,1,256]{2,1,0:T(1,128)} %reshape.312), calls=%async_computation.2 | async-start | bytes 8192 | tf_op jit(solution)/shard_map/all_to_all | solution.py:66
  60.5 1.1 %copy.39 = f32[16,8,4,256]{3,1,0,2:T(8,128)} copy(f32[16,8,4,256]{3,0,2,1:T(8,128)S(1)} %bitcast.23) | data formatting | bytes 1048576 | tf_op jit(solution)/shard_map/reshape | solution.py:54
  61.6 4.0 %all-to-all-done.2 = f32[4,1,256]{2,1,0:T(1,128)S(1)} async-done(((f32[4,1,256]{2,1,0:T(1,128)}), f32[4,1,256]{2,1,0:T(1,128)S(1)}, u32[]{:S(2)}, u32[]{:S(2)}) %all-to-all-start.2) | async-done | bytes 4128 | tf_op jit(solution)/shard_map/all_to_all | solution.py:66
  65.6 3.5 %all-to-all-start = ((f32[16,8,4,256]{3,1,0,2:T(8,128)}), f32[16,8,4,256]{3,1,0,2:T(8,128)S(1)}, u32[]{:S(2)}, u32[]{:S(2)}) async-start(f32[16,8,4,256]{3,1,0,2:T(8,128)} %copy.39), calls=%async_computation | async-start | bytes 1048576 | tf_op jit(solution)/shard_map/all_to_all | solution.py:59
  69.8 0.7 reduce.6
  70.6 0.7 reshape.314
  71.3 10.3 %all-to-all-done = f32[16,8,4,256]{3,1,0,2:T(8,128)S(1)} async-done(((f32[16,8,4,256]{3,1,0,2:T(8,128)}), f32[16,8,4,256]{3,1,0,2:T(8,128)S(1)}, u32[]{:S(2)}, u32[]{:S(2)}) %all-to-all-start) | async-done | bytes 524320 | tf_op jit(solution)/shard_map/all_to_all | solution.py:59
  81.6 3.6 %all-to-all-start.3 = ((f32[8,1,128]{2,1,0:T(1,128)}), f32[8,1,128]{2,1,0:T(1,128)S(1)}, u32[]{:S(2)}, u32[]{:S(2)}) async-start(f32[8,1,128]{2,1,0:T(1,128)} %reshape.314), calls=%async_computation.3 | async-start | bytes 8192 | tf_op jit(solution)/shard_map/all_to_all | solution.py:65
  85.2 1.1 %copy.40 = f32[16,8,4,256]{3,2,0,1:T(4,128)} copy(f32[16,8,4,256]{3,1,0,2:T(8,128)S(1)} %all-to-all-done) | data formatting | bytes 1048576 | tf_op jit(solution)/shard_map/all_to_all | solution.py:59
  86.4 3.5 %all-to-all-done.3 = f32[8,1,128]{2,1,0:T(1,128)S(1)} async-done(((f32[8,1,128]{2,1,0:T(1,128)}), f32[8,1,128]{2,1,0:T(1,128)S(1)}, u32[]{:S(2)}, u32[]{:S(2)}) %all-to-all-start.3) | async-done | bytes 4128 | tf_op jit(solution)/shard_map/all_to_all | solution.py:65
  89.8 3.5 %all-to-all-start.1 = ((f32[16,8,4,256]{3,2,0,1:T(4,128)}), f32[16,8,4,256]{3,2,0,1:T(4,128)S(1)}, u32[]{:S(2)}, u32[]{:S(2)}) async-start(f32[16,8,4,256]{3,2,0,1:T(4,128)} %copy.40), calls=%async_computation.1 | async-start | bytes 1048576 | tf_op jit(solution)/shard_map/all_to_all | solution.py:58
  93.7 0.7 reduce.7
  94.8 3.0 %scatter_custom_fusion.1 = s32[512]{0:T(512)} fusion(s32[512]{0:T(512)S(1)} %bitcast.30, s32[512]{0:T(512)S(1)} %bitcast.34, s32[]{:T(128)} %constant.107.clone.1), kind=kCustom, calls=%fused_computation.40 | custom fusion | bytes 2052 | tf_op jit(solution)/shard_map/scatter | solution.py:90
  97.8 3.0 %scatter_custom_fusion.2 = s32[512]{0:T(512)} fusion(s32[512]{0:T(512)S(1)} %bitcast.31, s32[512]{0:T(512)S(1)} %bitcast.33, s32[]{:T(128)} %constant.111.clone.1), kind=kCustom, calls=%fused_computation.38 | custom fusion | bytes 2052 | tf_op jit(solution)/shard_map/scatter | solution.py:95
  100.8 2.2 %all-to-all-done.1 = f32[16,8,4,256]{3,2,0,1:T(4,128)S(1)} async-done(((f32[16,8,4,256]{3,2,0,1:T(4,128)}), f32[16,8,4,256]{3,2,0,1:T(4,128)S(1)}, u32[]{:S(2)}, u32[]{:S(2)}) %all-to-all-start.1) | async-done | bytes 524320 | tf_op jit(solution)/shard_map/all_to_all | solution.py:58
  103.2 3.0 %scatter_custom_fusion = f32[512,256]{1,0:T(8,128)} fusion(s32[512]{0:T(512)S(1)} %bitcast.32, f32[512,256]{1,0:T(8,128)S(1)} %reshape.271, f32[]{:T(128)} %constant.100.clone.1), kind=kCustom, calls=%fused_computation.16 | custom fusion | bytes 524292 | tf_op jit(solution)/shard_map/scatter | solution.py:85
  (44 shorter events, 5.3 us)
Async XLA Ops:
  46.8 8.0 %copy-start = (s32[1,512]{1,0:T(1,128)S(1)}, s32[1,512]{1,0:T(1,128)}, u32[]{:S(2)}) copy-start(s32[1,512]{1,0:T(1,128)} %param.8) | copy-start | bytes 6148
  56.5 9.2 %all-to-all-start.2 = ((f32[4,1,256]{2,1,0:T(1,128)}), f32[4,1,256]{2,1,0:T(1,128)S(1)}, u32[]{:S(2)}, u32[]{:S(2)}) async-start(f32[4,1,256]{2,1,0:T(1,128)} %reshape.312), calls=%async_computation.2 | async-start | bytes 8192 | tf_op jit(solution)/shard_map/all_to_all | solution.py:66
  65.6 16.0 %all-to-all-start = ((f32[16,8,4,256]{3,1,0,2:T(8,128)}), f32[16,8,4,256]{3,1,0,2:T(8,128)S(1)}, u32[]{:S(2)}, u32[]{:S(2)}) async-start(f32[16,8,4,256]{3,1,0,2:T(8,128)} %copy.39), calls=%async_computation | async-start | bytes 1048576 | tf_op jit(solution)/shard_map/all_to_all | solution.py:59
  81.6 8.2 %all-to-all-start.3 = ((f32[8,1,128]{2,1,0:T(1,128)}), f32[8,1,128]{2,1,0:T(1,128)S(1)}, u32[]{:S(2)}, u32[]{:S(2)}) async-start(f32[8,1,128]{2,1,0:T(1,128)} %reshape.314), calls=%async_computation.3 | async-start | bytes 8192 | tf_op jit(solution)/shard_map/all_to_all | solution.py:65
  89.8 13.2 %all-to-all-start.1 = ((f32[16,8,4,256]{3,2,0,1:T(4,128)}), f32[16,8,4,256]{3,2,0,1:T(4,128)S(1)}, u32[]{:S(2)}, u32[]{:S(2)}) async-start(f32[16,8,4,256]{3,2,0,1:T(4,128)} %copy.40), calls=%async_computation.1 | async-start | bytes 1048576 | tf_op jit(solution)/shard_map/all_to_all | solution.py:58
where the time goes:
time: 107 us; the launch traced here: 106 us
  blocking collectives  42 us (39%)
  waiting for transfers between devices  20.1 us (19%)
  local copies, waits for them, and re-layouts  17.5 us (16%)
  starting transfers between devices  14.1 us (13%)
  matrix products  5.34 us (5%)
  other arithmetic  3.86 us (4%)
  between operations  3.41 us (3%)
    unnamed x1, blocking collectives  42 us
    all_to_all x1, waiting for transfers between devices, shards(): lax.all_to_all(outgoing[0], 'gz', split_axis=2, concat_axis=2, tiled=True)  10.3 us
    dot_general x2, matrix products, accumulate(): jnp.dot(hits.astype(jnp.float32), values, precision=lax.Precision.HIGHEST...  5.34 us
    all_to_all x1, waiting for transfers between devices, shards(): lax.all_to_all(outgoing[1], 'gz', split_axis=2, concat_axis=2, tiled=True)  4.02 us
    all_to_all x1, starting transfers between devices, shards(): lax.all_to_all(outgoing[1], 'gz', split_axis=2, concat_axis=2, tiled=True)  3.6 us
    all_to_all x1, starting transfers between devices, shards(): lax.all_to_all(lax.all_to_all(outgoing[1], 'gz', split_axis=2, concat_axi...  3.56 us
    all_to_all x1, starting transfers between devices, shards(): lax.all_to_all(lax.all_to_all(outgoing[0], 'gz', split_axis=2, concat_axi...  3.49 us
    all_to_all x1, starting transfers between devices, shards(): lax.all_to_all(outgoing[0], 'gz', split_axis=2, concat_axis=2, tiled=True)  3.47 us
  transfers between devices with their start and end apart: 4, of which 4 were waited for; matrix products, arithmetic and copies ran while one was open for 12% of the time, Pallas kernels for 0%

commit v1 on v0

--- a/solution.py
+++ b/solution.py
@@ -2,6 +2,18 @@
 import jax.numpy as jnp
 from jax import lax
 from jax.sharding import PartitionSpec as P
+
+
+def move_the_orders(inner_x, link_axis):
+    return jnp.concatenate(
+        lax.all_to_all(
+            jnp.stack(jnp.split(inner_x, lax.psum(1, axis_name=link_axis), axis=2), axis=0),
+            axis_name=link_axis,
+            split_axis=0,
+            concat_axis=0,
+        ),
+        axis=2,
+    )
 
 
 def shards(measures, group_index, distinct_keys, group_counts):
@@ -56,7 +68,7 @@
     outgoing = (arrange(sums), arrange(fields))
     arrived = (
         lax.all_to_all(
-            lax.all_to_all(outgoing[0], "gz", split_axis=2, concat_axis=2, tiled=True),
+            move_the_orders(outgoing[0], "gz"),
             ("gx", "gy"),
             split_axis=1,
             concat_axis=1,

time: 107 us -> 107 us (level)
    another operation x1 -> x3, local copies, waits for them, and re-layouts: 0.09 us -> 1.22 us  [the longest x2 1.14 us: move_the_orders(): jnp.stack(jnp.split(inner_x, lax.psum(1, axis_name=link_axis), axis=2), a...]
    all_to_all x2 -> x1, local copies, waits for them, and re-layouts: 1.18 us -> 0.04 us  [shards(): lax.all_to_all(move_the_orders(outgoing[0], 'gz'), ('gx', 'gy'), split_ax...]
    reshape x0 -> x1, local copies, waits for them, and re-layouts: none -> 1.14 us  [move_the_orders(): jnp.concatenate(lax.all_to_all(jnp.stack(jnp.split(inner_x, lax.psum(1, a...]
    reshape x2 -> x1, local copies, waits for them, and re-layouts: 1.11 us -> 0.01 us  [arrange(): return rolled.reshape((slots, plane, line) + array.shape[1:])]
where the time goes in v1:
time: 107 us; the launch traced here: 106 us
  blocking collectives  41.9 us (39%)
  waiting for transfers between devices  20 us (19%)
  local copies, waits for them, and re-layouts  17.5 us (16%)
  starting transfers between devices  14.1 us (13%)
  matrix products  5.34 us (5%)
  other arithmetic  3.89 us (4%)
  between operations  3.43 us (3%)
    unnamed x1, blocking collectives  41.9 us
    all_to_all x1, waiting for transfers between devices, move_the_orders(): lax.all_to_all(jnp.stack(jnp.split(inner_x, lax.psum(1, axis_name=link_ax...  10.3 us
    dot_general x2, matrix products, accumulate(): jnp.dot(hits.astype(jnp.float32), values, precision=lax.Precision.HIGHEST...  5.34 us
    all_to_all x1, waiting for transfers between devices, shards(): lax.all_to_all(outgoing[1], 'gz', split_axis=2, concat_axis=2, tiled=True)  3.93 us
    all_to_all x1, starting transfers between devices, shards(): lax.all_to_all(outgoing[1], 'gz', split_axis=2, concat_axis=2, tiled=True)  3.59 us
    all_to_all x1, starting transfers between devices, shards(): lax.all_to_all(lax.all_to_all(outgoing[1], 'gz', split_axis=2, concat_axi...  3.56 us
    all_to_all x1, starting transfers between devices, shards(): lax.all_to_all(move_the_orders(outgoing[0], 'gz'), ('gx', 'gy'), split_ax...  3.49 us
    all_to_all x1, starting transfers between devices, move_the_orders(): lax.all_to_all(jnp.stack(jnp.split(inner_x, lax.psum(1, axis_name=link_ax...  3.47 us
  transfers between devices with their start and end apart: 4, of which 4 were waited for; matrix products, arithmetic and copies ran while one was open for 12% of the time, Pallas kernels for 0%

profile of v1, /device:TPU:0, one launch (start us, length us, event | category | flops | bytes accessed | tf_op | source)
XLA Modules:
  0.0 106.3 jit_solution(5674813857012857537)
XLA Ops:
  1.4 41.9 %all-reduce = s32[32]{0:T(128)S(1)} all-reduce(s32[32]{0:T(128)S(1)} %dynamic-update-slice), channel_id=1, replica_groups=mesh['gx'=4,'gy'=2,'gz'=4] {'gx','gy','gz'}, use_global_device_ids=true, to_apply=%add | all-reduce | flops 32 | bytes 256
  46.8 7.4 %while.16 = (s32[]{:T(128)}, f32[512,256]{1,0:T(8,128)S(1)}, s32[512]{0:T(512)S(1)}, s32[2048]{0:T(1024)}, f32[2048,256]{1,0:T(8,128)}, /*index=5*/s32[]{:T(128)}, s32[]{:T(128)}, s32[]{:T(128)}, s32[]{:T(128)}) while((s32[]{:T(128)}, f32[512,256]{1,0:T(8,128)S(1)}, s32[512]{0:T(512)S(1)}, s32[2048]{0:T(1024)}, ...), condition=%wide.region_3.4_spmd.clone, body=%wide.region_1.3_spmd.clone.sunk | while | flops 1612972544 | bytes 2121886 | solution.py:51
  46.9 0.7 dynamic_slice.55
  47.5 2.7 %fusion.24 = f32[512,256]{1,0:T(8,128)S(1)} fusion(f32[2048,256]{1,0:T(8,128)} %get-tuple-element.207, s32[]{:T(128)S(6)} %select_n.107, s32[1024]{0:T(1024)S(1)} %dynamic_slice.55, f32[512,256]{1,0:T(8,128)S(1)} %get-tuple-element.195, pred[]{:T(512)S(6)} %compare.20), kind=kOutput, calls=%fused_computation.8.clone.1 | convolution fusion | flops 1611399168 | bytes 2101253 | tf_op jit(solution)/shard_map/while/body/eval_jaxpr/dot_general | solution.py:42
  50.5 0.7 dynamic_slice.55
  51.2 2.7 %fusion.24 = f32[512,256]{1,0:T(8,128)S(1)} fusion(f32[2048,256]{1,0:T(8,128)} %get-tuple-element.207, s32[]{:T(128)S(6)} %select_n.107, s32[1024]{0:T(1024)S(1)} %dynamic_slice.55, f32[512,256]{1,0:T(8,128)S(1)} %get-tuple-element.195, pred[]{:T(512)S(6)} %compare.20), kind=kOutput, calls=%fused_computation.8.clone.1 | convolution fusion | flops 1611399168 | bytes 2101253 | tf_op jit(solution)/shard_map/while/body/eval_jaxpr/dot_general | solution.py:42
  54.8 0.7 reduce.5
  55.8 0.7 reshape.320
  56.4 3.6 %all-to-all-start.2 = ((f32[4,1,256]{2,1,0:T(1,128)}), f32[4,1,256]{2,1,0:T(1,128)S(1)}, u32[]{:S(2)}, u32[]{:S(2)}) async-start(f32[4,1,256]{2,1,0:T(1,128)} %reshape.320), calls=%async_computation.2 | async-start | bytes 8192 | tf_op jit(solution)/shard_map/all_to_all | solution.py:78
  60.6 1.1 %copy.57 = f32[4,16,8,1,256]{4,2,1,3,0:T(8,128)} copy(f32[4,16,8,1,256]{4,1,2,3,0:T(8,128)S(1)} %pad_maximum_fusion) | data formatting | bytes 1048576 | tf_op jit(solution)/shard_map/stack | solution.py:10
  61.7 3.9 %all-to-all-done.2 = f32[4,1,256]{2,1,0:T(1,128)S(1)} async-done(((f32[4,1,256]{2,1,0:T(1,128)}), f32[4,1,256]{2,1,0:T(1,128)S(1)}, u32[]{:S(2)}, u32[]{:S(2)}) %all-to-all-start.2) | async-done | bytes 4128 | tf_op jit(solution)/shard_map/all_to_all | solution.py:78
  65.6 3.5 %all-to-all-start = ((f32[4,16,8,1,256]{4,2,1,3,0:T(8,128)}), f32[4,16,8,1,256]{4,2,1,3,0:T(8,128)S(1)}, u32[]{:S(2)}, u32[]{:S(2)}) async-start(f32[4,16,8,1,256]{4,2,1,3,0:T(8,128)} %copy.57), calls=%async_computation | async-start | bytes 1048576 | tf_op jit(solution)/shard_map/all_to_all | solution.py:9
  69.8 0.7 reduce.6
  70.6 0.7 reshape.322
  71.3 10.3 %all-to-all-done = f32[4,16,8,1,256]{4,2,1,3,0:T(8,128)S(1)} async-done(((f32[4,16,8,1,256]{4,2,1,3,0:T(8,128)}), f32[4,16,8,1,256]{4,2,1,3,0:T(8,128)S(1)}, u32[]{:S(2)}, u32[]{:S(2)}) %all-to-all-start) | async-done | bytes 524320 | tf_op jit(solution)/shard_map/all_to_all | solution.py:9
  81.6 3.6 %all-to-all-start.3 = ((f32[8,1,128]{2,1,0:T(1,128)}), f32[8,1,128]{2,1,0:T(1,128)S(1)}, u32[]{:S(2)}, u32[]{:S(2)}) async-start(f32[8,1,128]{2,1,0:T(1,128)} %reshape.322), calls=%async_computation.3 | async-start | bytes 8192 | tf_op jit(solution)/shard_map/all_to_all | solution.py:77
  85.2 1.1 %copy.58 = f32[16,8,4,256]{3,2,0,1:T(4,128)} copy(f32[16,8,4,256]{3,1,0,2:T(8,128)S(1)} %bitcast.40) | data formatting | bytes 1048576 | tf_op jit(solution)/shard_map/reshape | solution.py:8
  86.4 3.5 %all-to-all-done.3 = f32[8,1,128]{2,1,0:T(1,128)S(1)} async-done(((f32[8,1,128]{2,1,0:T(1,128)}), f32[8,1,128]{2,1,0:T(1,128)S(1)}, u32[]{:S(2)}, u32[]{:S(2)}) %all-to-all-start.3) | async-done | bytes 4128 | tf_op jit(solution)/shard_map/all_to_all | solution.py:77
  89.8 3.5 %all-to-all-start.1 = ((f32[16,8,4,256]{3,2,0,1:T(4,128)}), f32[16,8,4,256]{3,2,0,1:T(4,128)S(1)}, u32[]{:S(2)}, u32[]{:S(2)}) async-start(f32[16,8,4,256]{3,2,0,1:T(4,128)} %copy.58), calls=%async_computation.1 | async-start | bytes 1048576 | tf_op jit(solution)/shard_map/all_to_all | solution.py:70
  93.7 0.7 reduce.7
  94.8 3.0 %scatter_custom_fusion.1 = s32[512]{0:T(512)} fusion(s32[512]{0:T(512)S(1)} %bitcast.48, s32[512]{0:T(512)S(1)} %bitcast.52, s32[]{:T(128)} %constant.107.clone.1), kind=kCustom, calls=%fused_computation.45 | custom fusion | bytes 2052 | tf_op jit(solution)/shard_map/scatter | solution.py:102
  97.8 3.0 %scatter_custom_fusion.2 = s32[512]{0:T(512)} fusion(s32[512]{0:T(512)S(1)} %bitcast.49, s32[512]{0:T(512)S(1)} %bitcast.51, s32[]{:T(128)} %constant.111.clone.1), kind=kCustom, calls=%fused_computation.43 | custom fusion | bytes 2052 | tf_op jit(solution)/shard_map/scatter | solution.py:107
  100.8 2.2 %all-to-all-done.1 = f32[16,8,4,256]{3,2,0,1:T(4,128)S(1)} async-done(((f32[16,8,4,256]{3,2,0,1:T(4,128)}), f32[16,8,4,256]{3,2,0,1:T(4,128)S(1)}, u32[]{:S(2)}, u32[]{:S(2)}) %all-to-all-start.1) | async-done | bytes 524320 | tf_op jit(solution)/shard_map/all_to_all | solution.py:70
  103.2 3.0 %scatter_custom_fusion = f32[512,256]{1,0:T(8,128)} fusion(s32[512]{0:T(512)S(1)} %bitcast.50, f32[512,256]{1,0:T(8,128)S(1)} %reshape.279, f32[]{:T(128)} %constant.100.clone.1), kind=kCustom, calls=%fused_computation.17 | custom fusion | bytes 524292 | tf_op jit(solution)/shard_map/scatter | solution.py:97
  (46 shorter events, 5.4 us)
Async XLA Ops:
  46.8 8.0 %copy-start = (s32[1,512]{1,0:T(1,128)S(1)}, s32[1,512]{1,0:T(1,128)}, u32[]{:S(2)}) copy-start(s32[1,512]{1,0:T(1,128)} %param.8) | copy-start | bytes 6148
  56.4 9.2 %all-to-all-start.2 = ((f32[4,1,256]{2,1,0:T(1,128)}), f32[4,1,256]{2,1,0:T(1,128)S(1)}, u32[]{:S(2)}, u32[]{:S(2)}) async-start(f32[4,1,256]{2,1,0:T(1,128)} %reshape.320), calls=%async_computation.2 | async-start | bytes 8192 | tf_op jit(solution)/shard_map/all_to_all | solution.py:78
  65.6 16.0 %all-to-all-start = ((f32[4,16,8,1,256]{4,2,1,3,0:T(8,128)}), f32[4,16,8,1,256]{4,2,1,3,0:T(8,128)S(1)}, u32[]{:S(2)}, u32[]{:S(2)}) async-start(f32[4,16,8,1,256]{4,2,1,3,0:T(8,128)} %copy.57), calls=%async_computation | async-start | bytes 1048576 | tf_op jit(solution)/shard_map/all_to_all | solution.py:9
  81.6 8.2 %all-to-all-start.3 = ((f32[8,1,128]{2,1,0:T(1,128)}), f32[8,1,128]{2,1,0:T(1,128)S(1)}, u32[]{:S(2)}, u32[]{:S(2)}) async-start(f32[8,1,128]{2,1,0:T(1,128)} %reshape.322), calls=%async_computation.3 | async-start | bytes 8192 | tf_op jit(solution)/shard_map/all_to_all | solution.py:77
  89.8 13.2 %all-to-all-start.1 = ((f32[16,8,4,256]{3,2,0,1:T(4,128)}), f32[16,8,4,256]{3,2,0,1:T(4,128)S(1)}, u32[]{:S(2)}, u32[]{:S(2)}) async-start(f32[16,8,4,256]{3,2,0,1:T(4,128)} %copy.58), calls=%async_computation.1 | async-start | bytes 1048576 | tf_op jit(solution)/shard_map/all_to_all | solution.py:70
